TPU v7x, 32 devices: a whole 2x2x4 slice. The times are simulated.
32 devices in a mesh: surf: 8 (over y, x, core), probe: 4 (over z).
Axes of the slice: x: 2, y: 2, z: 4, core: 2. Of those that a mesh axis runs over, the one named last changes fastest.
Arguments:
- probes: bfloat16 [32, 65536], P('probe', 'surf'), may hold values from -6 to 6
- sigma: float32 [65536], P('surf'), may hold values from 0.5 to 2
- prior_patch: bfloat16 [128, 128], replicated, may hold values from -0.5 to 0.5
- owner_map: int32 [1024], P('surf'), may hold values from 0 to 7, as said below
- block_perm: int32 [1024], P('surf'), may hold values from 0 to 127, as said below
- col_counts: int32 [1024], P('surf'), may hold values from 1 to 64
- coef: bfloat16 [1024, 1024], P('surf'), may hold values from 0.5 to 1.5
- obs_weight: bfloat16 [1024, 64], P('surf'), may hold values from 0.25 to 1
- column_op: bfloat16 [1024, 1024], replicated, may hold values from -0.1875 to 0.1875
Outputs:
- hess: float32 [32, 65536], P('probe', 'surf')
- diag_est: float32 [65536], P('surf')
- quad: float32 [32], P('probe')
Inputs may be any that keep to these rules, and one draw needn't show every extreme that they name: `owner_map`: the 128 blocks of each surface device go to 8 different column owners, 16 to each. The pairs (owner_map, block_perm) name every slot of every column owner exactly once; a column owner receives 16 blocks from each of 8 surface devices.
All inputs are finite; a program needn't handle non-finite values.
Results may differ from a plain program's by a relative error of at most 0.005.
Values may be sent and summed in bfloat16 or wider, within the bound.
No kernel may reach another device: no remote copies, remote signals or barrier semaphores. Data moves between devices by JAX's collectives and lax.ppermute only.
A program may use at most 64 MiB of HBM per device.

v0:
```python
import jax
import jax.numpy as jnp
from jax import lax
from jax.sharding import PartitionSpec as P

P_SIZE = 32
BS = 64
PATCH = 128


def column_term(fields, coef_rows, obs_rows, counts, valid, column_op):
    rows, width, cols = fields.shape
    layers = coef_rows.shape[1] // cols
    column = lax.broadcasted_iota(jnp.int32, (rows, cols), 1)
    keep = jnp.where((column < counts[:, None]) & valid[:, None], 1.0, 0.0).astype(jnp.float32)
    coef_full = (
        coef_rows.astype(jnp.float32).reshape(rows, 1, layers, cols) * keep[:, None, None, :]
    )
    lifted = (fields.astype(jnp.float32)[:, :, None, :] * coef_full).astype(jnp.bfloat16)
    state = jnp.dot(
        lifted.reshape(rows * width, layers * cols), column_op, preferred_element_type=jnp.float32
    )
    weighted = (
        state.reshape(rows, width, layers, cols) * obs_rows.astype(jnp.float32)[:, None, None, :]
    ).astype(jnp.bfloat16)
    adjoint = lax.dot_general(
        weighted.reshape(rows * width, layers * cols),
        column_op,
        (((1,), (1,)), ((), ())),
        preferred_element_type=jnp.float32,
    )
    return jnp.sum(adjoint.reshape(rows, width, layers, cols) * coef_full, axis=2)


def body(
    probes, sigma, prior_patch, owner_map, block_perm, col_counts, coef, obs_weight, column_op
):
    width, nodes = probes.shape
    blocks = owner_map.shape[0]
    peers = lax.axis_size("surf")
    depth = max(1, blocks // peers)
    slots_all = peers * depth
    grouped = probes.reshape(width, nodes // PATCH, PATCH)
    mixed = jnp.einsum("pki,ij->pkj", grouped, prior_patch, preferred_element_type=jnp.float32)
    spread = (mixed.reshape(width, nodes) * sigma[None, :]).astype(jnp.bfloat16)
    fields = spread.reshape(width, blocks, BS).transpose(1, 0, 2)
    row_ids = lax.broadcasted_iota(jnp.int32, (blocks, blocks), 0)
    col_ids = lax.broadcasted_iota(jnp.int32, (blocks, blocks), 1)
    same = (owner_map[None, :] == owner_map[:, None]) & (col_ids < row_ids)
    rank = jnp.sum(same.astype(jnp.int32), axis=1)
    position = owner_map * depth + rank
    request = (
        jnp.full((slots_all,), -1, jnp.int32).at[position].set(block_perm).reshape(peers, depth)
    )
    asked = lax.all_to_all(request, "surf", split_axis=0, concat_axis=0, tiled=True)
    wanted = asked >= 0
    safe_asked = jnp.maximum(asked, 0)
    coef_out = jnp.where(wanted[:, :, None], coef[safe_asked], jnp.zeros((), jnp.bfloat16))
    obs_out = jnp.where(wanted[:, :, None], obs_weight[safe_asked], jnp.zeros((), jnp.bfloat16))
    coef_in, obs_in = (
        lax.all_to_all(coef_out, "surf", split_axis=0, concat_axis=0, tiled=True),
        lax.all_to_all(obs_out, "surf", split_axis=0, concat_axis=0, tiled=True),
    )
    coef_rows = coef_in.reshape(slots_all, coef.shape[1])[position]
    obs_rows = obs_in.reshape(slots_all, BS)[position]
    everyone = jnp.ones((blocks,), dtype=bool)
    sens = column_term(fields, coef_rows, obs_rows, col_counts, everyone, column_op)
    sens = sens.transpose(1, 0, 2).reshape(width, nodes)
    scaled = (sens * sigma[None, :]).reshape(width, nodes // PATCH, PATCH)
    back = jnp.einsum(
        "pkj,ij->pki", scaled, prior_patch.astype(jnp.float32), precision=lax.Precision.HIGHEST
    ).reshape(width, nodes)
    values = probes.astype(jnp.float32)
    hess = values + back
    product = values * back
    diag_est = lax.psum(jnp.sum(product, axis=0), "probe") / P_SIZE
    quad = lax.psum(jnp.sum(product, axis=1), "surf")
    return (hess, diag_est, quad)


def solution(mesh):
    in_specs = (
        P("probe", "surf"),
        P("surf"),
        P(),
        P("surf"),
        P("surf"),
        P("surf"),
        P("surf", None),
        P("surf", None),
        P(),
    )
    out_specs = (P("probe", "surf"), P("surf"), P("probe"))
    return jax.shard_map(body, mesh=mesh, in_specs=in_specs, out_specs=out_specs, check_vma=False)
```

profile of v0, /device:TPU:0, one launch (start us, length us, event | category | flops | bytes accessed | tf_op | source)
XLA Modules:
  0.0 75.5 jit_solution(10636901468613469254)
XLA Ops:
  0.7 0.9 %convert_reduce_fusion = s32[128]{0:T(128)S(1)} fusion(s32[128]{0:T(128)} %param.12), kind=kLoop, calls=%fused_computation.21 | loop fusion | flops 81792 | bytes 1024 | tf_op jit(solution)/shard_map/reduce_sum | solution.py:50
  2.2 1.1 %scatter_custom_fusion = s32[128]{0:T(128)S(1)} fusion(s32[128]{0:T(128)S(1)} %compare_select_fusion, s32[128]{0:T(128)} %param.13, s32[]{:T(128)} %constant.8.clone.1), kind=kCustom, calls=%fused_computation.35 | custom fusion | bytes 1024 | tf_op jit(solution)/shard_map/scatter | solution.py:53
  4.0 5.2 %all-to-all-start = ((s32[8,1,16]{2,1,0:T(1,128)}), s32[8,1,16]{2,1,0:T(1,128)S(1)}, u32[]{:S(2)}, u32[]{:S(2)}) async-start(s32[8,1,16]{2,1,0:T(1,128)} %bitcast.3), calls=%async_computation | async-start | bytes 8192 | tf_op jit(solution)/shard_map/all_to_all | solution.py:55
  9.2 0.8 %mul.80 = f32[128,64]{1,0:T(8,128)S(1)} reshape(f32[8192]{0:T(1024)} %param.10) | data formatting | bytes 65536 | tf_op jit(solution)/shard_map/mul | solution.py:45
  10.0 1.1 %fusion.3 = f32[8,64,128]{2,1,0:T(8,128)S(1)} fusion(bf16[8,64,128]{2,0,1:T(8,128)(2,1)} %bitcast.61, bf16[128,128]{1,0:T(8,128)(2,1)} %param.11), kind=kOutput, calls=%fused_computation.18 | convolution fusion | flops 16777216 | bytes 425984 | tf_op jit(solution)/shard_map/pki,ij->pkj/dot_general | solution.py:44
  11.5 2.4 %all-to-all-done = s32[8,1,16]{2,1,0:T(1,128)S(1)} async-done(((s32[8,1,16]{2,1,0:T(1,128)}), s32[8,1,16]{2,1,0:T(1,128)S(1)}, u32[]{:S(2)}, u32[]{:S(2)}) %all-to-all-start) | async-done | bytes 544 | tf_op jit(solution)/shard_map/all_to_all | solution.py:55
  13.9 0.7 gather_fusion.2
  14.7 0.7 reshape.188
  15.4 3.3 %all-to-all-start.2 = ((bf16[8,2,512]{2,1,0:T(2,128)(2,1)}), bf16[8,2,512]{2,1,0:T(2,128)(2,1)S(1)}, u32[]{:S(2)}, u32[]{:S(2)}) async-start(bf16[8,2,512]{2,1,0:T(2,128)(2,1)} %reshape.188), calls=%async_computation.2 | async-start | bytes 32768 | tf_op jit(solution)/shard_map/all_to_all | solution.py:62
  18.8 0.9 %gather_fusion = bf16[128,1024]{1,0:T(8,128)(2,1)S(1)} fusion(bf16[128,1024]{1,0:T(8,128)(2,1)S(1)} %copy-done, s32[1024]{0:T(1024)S(1)} %pad_clamp_fusion.1), kind=kCustom, calls=%fused_computation | custom fusion | bytes 524800 | tf_op jit(solution)/shard_map/gather | solution.py:58
  19.7 0.8 %broadcast_select_fusion = bf16[8,16,1024]{2,1,0:T(8,128)(2,1)} fusion(bf16[8,16,1024]{2,1,0:T(8,128)(2,1)S(1)} %bitcast.60, pred[8,16]{1,0:T(8,128)(4,1)S(1)} %compare_bitcast_fusion), kind=kLoop, calls=%fused_computation.15 | loop fusion | flops 131072 | bytes 524416 | tf_op jit(solution)/shard_map/jit(_where)/select_n | solution.py:58
  20.5 3.0 %all-to-all-done.2 = bf16[8,2,512]{2,1,0:T(2,128)(2,1)S(1)} async-done(((bf16[8,2,512]{2,1,0:T(2,128)(2,1)}), bf16[8,2,512]{2,1,0:T(2,128)(2,1)S(1)}, u32[]{:S(2)}, u32[]{:S(2)}) %all-to-all-start.2) | async-done | bytes 16416 | tf_op jit(solution)/shard_map/all_to_all | solution.py:62
  23.5 3.4 %all-to-all-start.1 = ((bf16[8,16,1024]{2,1,0:T(8,128)(2,1)}), bf16[8,16,1024]{2,1,0:T(8,128)(2,1)S(1)}, u32[]{:S(2)}, u32[]{:S(2)}) async-start(bf16[8,16,1024]{2,1,0:T(8,128)(2,1)} %broadcast_select_fusion), calls=%async_computation.1 | async-start | bytes 524288 | tf_op jit(solution)/shard_map/all_to_all | solution.py:61
  26.9 0.9 %copy.53 = f32[128,8,64]{0,2,1:T(8,128)} copy(f32[128,8,64]{2,0,1:T(8,128)S(1)} %convert_bitcast_fusion) | data formatting | bytes 524288 | tf_op jit(solution)/shard_map/convert_element_type | solution.py:19
  27.8 2.6 %copy.58 = bf16[1024,1024]{0,1:T(8,128)(2,1)} copy(bf16[1024,1024]{1,0:T(8,128)(2,1)S(1)} %copy-done.1) | data formatting | bytes 4194304 | tf_op args[8]
  30.5 0.7 gather_fusion.3
  31.3 2.4 %all-to-all-done.1 = bf16[8,16,1024]{2,1,0:T(8,128)(2,1)S(1)} async-done(((bf16[8,16,1024]{2,1,0:T(8,128)(2,1)}), bf16[8,16,1024]{2,1,0:T(8,128)(2,1)S(1)}, u32[]{:S(2)}, u32[]{:S(2)}) %all-to-all-start.1) | async-done | bytes 262176 | tf_op jit(solution)/shard_map/all_to_all | solution.py:61
  33.7 0.9 %gather_fusion.1 = bf16[128,1024]{1,0:T(8,128)(2,1)S(1)} fusion(bf16[128,1024]{1,0:T(8,128)(2,1)S(1)} %bitcast.54, s32[1024]{0:T(1024)S(1)} %pad_clamp_fusion), kind=kCustom, calls=%fused_computation.1 | custom fusion | bytes 524800 | tf_op jit(solution)/shard_map/gather | solution.py:64
  34.8 1.7 %multiply_convert_fusion.1 = bf16[128,8,16,64]{0,3,2,1:T(8,128)(2,1)S(1)} fusion(f32[128,16,64]{0,2,1:T(8,128)S(1)} %broadcast_multiply_fusion, f32[128,8,64]{0,2,1:T(8,128)} %copy.53), kind=kLoop, calls=%fused_computation.7 | loop fusion | flops 2097152 | bytes 2883584 | tf_op jit(solution)/shard_map/convert_element_type | solution.py:19
  36.5 2.4 %multiply_convert_fusion = bf16[128,8,16,64]{0,3,2,1:T(8,128)(2,1)S(1)} fusion(bf16[128,8,1024,1]{0,2,3,1:T(8,128)(2,1)S(1)} %bitcast.58, bf16[16,64,1024,1]{2,1,0,3:T(8,128)(2,1)S(1)} %bitcast.57, f32[128,64]{0,1:T(8,128)S(1)} %convert_element_type.61), kind=kOutput, calls=%fused_computation.6 | convolution fusion | flops 2149580800 | bytes 6324224 | tf_op jit(solution)/shard_map/dot_general | solution.py:20
  38.9 2.4 %multiply_reduce_fusion = f32[128,8,64]{0,2,1:T(8,128)S(1)} fusion(bf16[128,8,1024,1]{0,2,3,1:T(8,128)(2,1)S(1)} %bitcast.67, bf16[16,64,1024,1]{2,1,0,3:T(8,128)(2,1)S(1)} %bitcast.56, f32[128,16,64]{0,2,1:T(8,128)S(1)} %broadcast_multiply_fusion), kind=kOutput, calls=%fused_computation.5 | convolution fusion | flops 2149515264 | bytes 4980736 | tf_op jit(solution)/shard_map/dot_general | solution.py:26
  42.2 1.0 %fusion.1 = (f32[8]{0:T(128)S(1)}, f32[8192]{0:T(1024)S(1)}, f32[8,8192]{1,0:T(8,128)}) fusion(f32[1,8,64,128]{3,2,1,0:T(8,128)S(1)} %convolution_bitcast_fusion, bf16[8,8192]{1,0:T(8,128)(2,1)S(1)} %copy-done.3), kind=kLoop, calls=%fused_computation.16 | loop fusion | flops 319480 | bytes 688160 | tf_op jit(solution)/shard_map/reduce_sum | solution.py:77
  43.2 12.4 %psum.15 = f32[8]{0:T(128)} all-reduce(f32[8]{0:T(128)S(1)} %get-tuple-element.3), channel_id=1, replica_groups=mesh['surf'=8,'probe'=4] {'surf'}, use_global_device_ids=true, to_apply=%region_6.7 | all-reduce | flops 8 | bytes 64 | tf_op jit(solution)/shard_map/psum | solution.py:77
  55.6 19.3 %psum.14 = f32[8192]{0:T(1024)S(1)} all-reduce(f32[8192]{0:T(1024)S(1)} %get-tuple-element.4), channel_id=1, replica_groups=mesh['surf'=8,'probe'=4] {'probe'}, use_global_device_ids=true, to_apply=%region_4.5 | all-reduce | flops 8192 | bytes 65536 | tf_op jit(solution)/shard_map/psum | solution.py:76
  (37 shorter events, 3.7 us)
Async XLA Ops:
  0.6 18.2 %copy-start = (bf16[128,1024]{1,0:T(8,128)(2,1)S(1)}, bf16[128,1024]{1,0:T(8,128)(2,1)}, u32[]{:S(2)}) copy-start(bf16[128,1024]{1,0:T(8,128)(2,1)} %param.15) | copy-start | bytes 786436
  0.6 10.7 %copy-start.6 = (bf16[128,64]{0,1:T(8,128)(2,1)S(1)}, bf16[128,64]{0,1:T(8,128)(2,1)}, u32[]{:S(2)}) copy-start(bf16[128,64]{0,1:T(8,128)(2,1)} %param.16) | copy-start | bytes 49156
  4.0 9.8 %all-to-all-start = ((s32[8,1,16]{2,1,0:T(1,128)}), s32[8,1,16]{2,1,0:T(1,128)S(1)}, u32[]{:S(2)}, u32[]{:S(2)}) async-start(s32[8,1,16]{2,1,0:T(1,128)} %bitcast.3), calls=%async_computation | async-start | bytes 8192 | tf_op jit(solution)/shard_map/all_to_all | solution.py:55
  15.4 8.0 %all-to-all-start.2 = ((bf16[8,2,512]{2,1,0:T(2,128)(2,1)}), bf16[8,2,512]{2,1,0:T(2,128)(2,1)S(1)}, u32[]{:S(2)}, u32[]{:S(2)}) async-start(bf16[8,2,512]{2,1,0:T(2,128)(2,1)} %reshape.188), calls=%async_computation.2 | async-start | bytes 32768 | tf_op jit(solution)/shard_map/all_to_all | solution.py:62
  18.8 9.0 %copy-start.1 = (bf16[1024,1024]{1,0:T(8,128)(2,1)S(1)}, bf16[1024,1024]{1,0:T(8,128)(2,1)}, u32[]{:S(2)}) copy-start(bf16[1024,1024]{1,0:T(8,128)(2,1)} %param.17) | copy-start | bytes 6291460
  23.5 10.3 %all-to-all-start.1 = ((bf16[8,16,1024]{2,1,0:T(8,128)(2,1)}), bf16[8,16,1024]{2,1,0:T(8,128)(2,1)S(1)}, u32[]{:S(2)}, u32[]{:S(2)}) async-start(bf16[8,16,1024]{2,1,0:T(8,128)(2,1)} %broadcast_select_fusion), calls=%async_computation.1 | async-start | bytes 524288 | tf_op jit(solution)/shard_map/all_to_all | solution.py:61
  27.8 2.6 %copy-start.7 = (s32[128]{0:T(128)S(1)}, s32[128]{0:T(128)}, u32[]{:S(2)}) copy-start(s32[128]{0:T(128)} %param.14) | copy-start | bytes 1540
  34.7 1.7 %copy-start.2 = (bf16[1024,1024]{0,1:T(8,128)(2,1)S(1)}, bf16[1024,1024]{0,1:T(8,128)(2,1)}, u32[]{:S(2)}) copy-start(bf16[1024,1024]{0,1:T(8,128)(2,1)} %copy.58) | copy-start | bytes 6291460
  38.8 2.8 %copy-start.4 = (f32[8192]{0:T(1024)S(1)}, f32[8192]{0:T(1024)}, u32[]{:S(2)}) copy-start(f32[8192]{0:T(1024)} %param.10) | copy-start | bytes 98308
  38.9 2.8 %copy-start.5 = (bf16[128,128]{1,0:T(8,128)(2,1)S(1)}, bf16[128,128]{1,0:T(8,128)(2,1)}, u32[]{:S(2)}) copy-start(bf16[128,128]{1,0:T(8,128)(2,1)} %param.11) | copy-start | bytes 98308
  41.3 0.9 %copy-start.3 = (bf16[8,8192]{1,0:T(8,128)(2,1)S(1)}, bf16[8,8192]{1,0:T(8,128)(2,1)}, u32[]{:S(2)}) copy-start(bf16[8,8192]{1,0:T(8,128)(2,1)} %param.9) | copy-start | bytes 393220
where the time goes:
time: 76.1 us; the launch traced here: 75.5 us
  blocking collectives  31.8 us (42%)
  starting transfers between devices  11.9 us (16%)
  local copies, waits for them, and re-layouts  11.2 us (15%)
  waiting for transfers between devices  7.81 us (10%)
  matrix products  6.1 us (8%)
  other arithmetic  5.83 us (8%)
  between operations  0.9 us (1%)
    psum x1, blocking collectives, body(): diag_est = lax.psum(jnp.sum(product, axis=0), 'probe') / P_SIZE  19.3 us
    psum x1, blocking collectives, body(): quad = lax.psum(jnp.sum(product, axis=1), 'surf')  12.4 us
    all_to_all x1, starting transfers between devices, body(): lax.all_to_all(request, 'surf', split_axis=0, concat_axis=0, tiled=True)  5.2 us
    unnamed x20, local copies, waits for them, and re-layouts  3.75 us
    all_to_all x1, starting transfers between devices, body(): lax.all_to_all(coef_out, 'surf', split_axis=0, concat_axis=0, tiled=True)  3.41 us
    all_to_all x1, starting transfers between devices, body(): lax.all_to_all(obs_out, 'surf', split_axis=0, concat_axis=0, tiled=True)  3.34 us
    all_to_all x1, waiting for transfers between devices, body(): lax.all_to_all(obs_out, 'surf', split_axis=0, concat_axis=0, tiled=True)  3.01 us
    all_to_all x1, waiting for transfers between devices, body(): lax.all_to_all(coef_out, 'surf', split_axis=0, concat_axis=0, tiled=True)  2.43 us
  transfers between devices with their start and end apart: 3, of which 3 were waited for; matrix products, arithmetic and copies ran while one was open for 11% of the time, Pallas kernels for 0%

commit v1 on v0

--- a/solution.py
+++ b/solution.py
@@ -30,6 +30,29 @@
         preferred_element_type=jnp.float32,
     )
     return jnp.sum(adjoint.reshape(rows, width, layers, cols) * coef_full, axis=2)
+
+
+def total_over(part, axis):
+    size = lax.axis_size(axis)
+    total = part
+    for shift in range(size - 1, 0, -1):
+        total = total + lax.ppermute(part, axis, [(i, partner(i, shift, size)) for i in range(size)])
+    return total
+
+
+def partner(i, shift, size):
+    return i ^ shift if size & (size - 1) == 0 else (i + shift) % size
+
+
+def halving_sum(part, axis):
+    size = lax.axis_size(axis)
+    if size & (size - 1):
+        return lax.psum(part, axis)
+    step = 1
+    while step < size:
+        part = part + lax.ppermute(part, axis, [(i, i ^ step) for i in range(size)])
+        step *= 2
+    return part
 
 
 def body(
@@ -73,8 +96,8 @@
     values = probes.astype(jnp.float32)
     hess = values + back
     product = values * back
-    diag_est = lax.psum(jnp.sum(product, axis=0), "probe") / P_SIZE
-    quad = lax.psum(jnp.sum(product, axis=1), "surf")
+    diag_est = total_over(jnp.sum(product, axis=0), "probe") / P_SIZE
+    quad = halving_sum(jnp.sum(product, axis=1), "surf")
     return (hess, diag_est, quad)
 
 

time: 76.1 us -> 57.5 us (0.76)
  blocking collectives: 31.8 us -> 0 us
  waiting for transfers between devices: 7.81 us -> 15.1 us
  starting transfers between devices: 11.9 us -> 17.5 us
    psum x2 -> x0, blocking collectives: 31.8 us -> none  [the longest x1 19.3 us: body(): diag_est = lax.psum(jnp.sum(product, axis=0), 'probe') / P_SIZE]
    ppermute x0 -> x6, waiting for transfers between devices: none -> 7.21 us  [the longest x3 7.2 us: halving_sum(): part = part + lax.ppermute(part, axis, [(i, i ^ step) for i in range(size)])]
    ppermute x0 -> x6, starting transfers between devices: none -> 5.54 us  [the longest x3 4.44 us: total_over(): lax.ppermute(part, axis, [(i, partner(i, shift, size)) for i in range(siz...]
  transfers between devices with their start and end apart: 3 -> 9, of which waited for: 3 -> 6; matrix products, arithmetic and copies ran while one was open for 11% -> 15% of each run, Pallas kernels for 0% -> 0%
where the time goes in v1:
time: 57.5 us; the launch traced here: 57.1 us
  starting transfers between devices  17.5 us (30%)
  waiting for transfers between devices  15.1 us (26%)
  local copies, waits for them, and re-layouts  11.2 us (19%)
  other arithmetic  6.35 us (11%)
  matrix products  6.1 us (11%)
  between operations  0.91 us (2%)
    ppermute x3, waiting for transfers between devices, halving_sum(): part = part + lax.ppermute(part, axis, [(i, i ^ step) for i in range(size)])  7.2 us
    all_to_all x1, starting transfers between devices, body(): lax.all_to_all(request, 'surf', split_axis=0, concat_axis=0, tiled=True)  5.2 us
    ppermute x3, starting transfers between devices, total_over(): lax.ppermute(part, axis, [(i, partner(i, shift, size)) for i in range(siz...  4.44 us
    unnamed x20, local copies, waits for them, and re-layouts  3.74 us
    all_to_all x1, starting transfers between devices, body(): lax.all_to_all(coef_out, 'surf', split_axis=0, concat_axis=0, tiled=True)  3.41 us
    all_to_all x1, starting transfers between devices, body(): lax.all_to_all(obs_out, 'surf', split_axis=0, concat_axis=0, tiled=True)  3.34 us
    all_to_all x1, waiting for transfers between devices, body(): lax.all_to_all(obs_out, 'surf', split_axis=0, concat_axis=0, tiled=True)  3.01 us
    all_to_all x1, waiting for transfers between devices, body(): lax.all_to_all(coef_out, 'surf', split_axis=0, concat_axis=0, tiled=True)  2.47 us
  transfers between devices with their start and end apart: 9, of which 6 were waited for; matrix products, arithmetic and copies ran while one was open for 15% of the time, Pallas kernels for 0%

profile of v1, /device:TPU:0, one launch (start us, length us, event | category | flops | bytes accessed | tf_op | source)
XLA Modules:
  0.0 57.1 jit_solution(18037170820837944603)
XLA Ops:
  0.7 0.9 %convert_reduce_fusion = s32[128]{0:T(128)S(1)} fusion(s32[128]{0:T(128)} %param.12), kind=kLoop, calls=%fused_computation.21 | loop fusion | flops 81792 | bytes 1024 | tf_op jit(solution)/shard_map/reduce_sum | solution.py:73
  2.2 1.1 %scatter_custom_fusion = s32[128]{0:T(128)S(1)} fusion(s32[128]{0:T(128)S(1)} %compare_select_fusion, s32[128]{0:T(128)} %param.13, s32[]{:T(128)} %constant.8.clone.1), kind=kCustom, calls=%fused_computation.35 | custom fusion | bytes 1024 | tf_op jit(solution)/shard_map/scatter | solution.py:76
  4.0 5.2 %all-to-all-start = ((s32[8,1,16]{2,1,0:T(1,128)}), s32[8,1,16]{2,1,0:T(1,128)S(1)}, u32[]{:S(2)}, u32[]{:S(2)}) async-start(s32[8,1,16]{2,1,0:T(1,128)} %bitcast.3), calls=%async_computation | async-start | bytes 8192 | tf_op jit(solution)/shard_map/all_to_all | solution.py:78
  9.2 0.8 %mul.80 = f32[128,64]{1,0:T(8,128)S(1)} reshape(f32[8192]{0:T(1024)} %param.10) | data formatting | bytes 65536 | tf_op jit(solution)/shard_map/mul | solution.py:68
  10.0 1.1 %fusion.3 = f32[8,64,128]{2,1,0:T(8,128)S(1)} fusion(bf16[8,64,128]{2,0,1:T(8,128)(2,1)} %bitcast.61, bf16[128,128]{1,0:T(8,128)(2,1)} %param.11), kind=kOutput, calls=%fused_computation.18 | convolution fusion | flops 16777216 | bytes 425984 | tf_op jit(solution)/shard_map/pki,ij->pkj/dot_general | solution.py:67
  11.5 2.4 %all-to-all-done = s32[8,1,16]{2,1,0:T(1,128)S(1)} async-done(((s32[8,1,16]{2,1,0:T(1,128)}), s32[8,1,16]{2,1,0:T(1,128)S(1)}, u32[]{:S(2)}, u32[]{:S(2)}) %all-to-all-start) | async-done | bytes 544 | tf_op jit(solution)/shard_map/all_to_all | solution.py:78
  15.4 3.3 %all-to-all-start.2 = ((bf16[8,2,512]{2,1,0:T(2,128)(2,1)}), bf16[8,2,512]{2,1,0:T(2,128)(2,1)S(1)}, u32[]{:S(2)}, u32[]{:S(2)}) async-start(bf16[8,2,512]{2,1,0:T(2,128)(2,1)} %reshape.188), calls=%async_computation.2 | async-start | bytes 32768 | tf_op jit(solution)/shard_map/all_to_all | solution.py:85
  18.8 0.9 %gather_fusion = bf16[128,1024]{1,0:T(8,128)(2,1)S(1)} fusion(bf16[128,1024]{1,0:T(8,128)(2,1)S(1)} %copy-done, s32[1024]{0:T(1024)S(1)} %pad_clamp_fusion.1), kind=kCustom, calls=%fused_computation | custom fusion | bytes 524800 | tf_op jit(solution)/shard_map/gather | solution.py:81
  19.7 0.8 %broadcast_select_fusion = bf16[8,16,1024]{2,1,0:T(8,128)(2,1)} fusion(bf16[8,16,1024]{2,1,0:T(8,128)(2,1)S(1)} %bitcast.60, pred[8,16]{1,0:T(8,128)(4,1)S(1)} %compare_bitcast_fusion), kind=kLoop, calls=%fused_computation.15 | loop fusion | flops 131072 | bytes 524416 | tf_op jit(solution)/shard_map/jit(_where)/select_n | solution.py:81
  20.5 3.0 %all-to-all-done.2 = bf16[8,2,512]{2,1,0:T(2,128)(2,1)S(1)} async-done(((bf16[8,2,512]{2,1,0:T(2,128)(2,1)}), bf16[8,2,512]{2,1,0:T(2,128)(2,1)S(1)}, u32[]{:S(2)}, u32[]{:S(2)}) %all-to-all-start.2) | async-done | bytes 16416 | tf_op jit(solution)/shard_map/all_to_all | solution.py:85
  23.5 3.4 %all-to-all-start.1 = ((bf16[8,16,1024]{2,1,0:T(8,128)(2,1)}), bf16[8,16,1024]{2,1,0:T(8,128)(2,1)S(1)}, u32[]{:S(2)}, u32[]{:S(2)}) async-start(bf16[8,16,1024]{2,1,0:T(8,128)(2,1)} %broadcast_select_fusion), calls=%async_computation.1 | async-start | bytes 524288 | tf_op jit(solution)/shard_map/all_to_all | solution.py:84
  26.9 0.9 %copy.53 = f32[128,8,64]{0,2,1:T(8,128)} copy(f32[128,8,64]{2,0,1:T(8,128)S(1)} %convert_bitcast_fusion) | data formatting | bytes 524288 | tf_op jit(solution)/shard_map/convert_element_type | solution.py:19
  27.8 2.5 %copy.58 = bf16[1024,1024]{0,1:T(8,128)(2,1)} copy(bf16[1024,1024]{1,0:T(8,128)(2,1)S(1)} %copy-done.1) | data formatting | bytes 4194304 | tf_op args[8]
  31.3 2.5 %all-to-all-done.1 = bf16[8,16,1024]{2,1,0:T(8,128)(2,1)S(1)} async-done(((bf16[8,16,1024]{2,1,0:T(8,128)(2,1)}), bf16[8,16,1024]{2,1,0:T(8,128)(2,1)S(1)}, u32[]{:S(2)}, u32[]{:S(2)}) %all-to-all-start.1) | async-done | bytes 262176 | tf_op jit(solution)/shard_map/all_to_all | solution.py:84
  33.7 0.9 %gather_fusion.1 = bf16[128,1024]{1,0:T(8,128)(2,1)S(1)} fusion(bf16[128,1024]{1,0:T(8,128)(2,1)S(1)} %bitcast.54, s32[1024]{0:T(1024)S(1)} %pad_clamp_fusion), kind=kCustom, calls=%fused_computation.1 | custom fusion | bytes 524800 | tf_op jit(solution)/shard_map/gather | solution.py:87
  34.8 1.7 %multiply_convert_fusion.1 = bf16[128,8,16,64]{0,3,2,1:T(8,128)(2,1)S(1)} fusion(f32[128,16,64]{0,2,1:T(8,128)S(1)} %broadcast_multiply_fusion, f32[128,8,64]{0,2,1:T(8,128)} %copy.53), kind=kLoop, calls=%fused_computation.7 | loop fusion | flops 2097152 | bytes 2883584 | tf_op jit(solution)/shard_map/convert_element_type | solution.py:19
  36.5 2.4 %multiply_convert_fusion = bf16[128,8,16,64]{0,3,2,1:T(8,128)(2,1)S(1)} fusion(bf16[128,8,1024,1]{0,2,3,1:T(8,128)(2,1)S(1)} %bitcast.58, bf16[16,64,1024,1]{2,1,0,3:T(8,128)(2,1)S(1)} %bitcast.57, f32[128,64]{0,1:T(8,128)S(1)} %convert_element_type.61), kind=kOutput, calls=%fused_computation.6 | convolution fusion | flops 2149580800 | bytes 6324224 | tf_op jit(solution)/shard_map/dot_general | solution.py:20
  38.9 2.4 %multiply_reduce_fusion = f32[128,8,64]{0,2,1:T(8,128)S(1)} fusion(bf16[128,8,1024,1]{0,2,3,1:T(8,128)(2,1)S(1)} %bitcast.67, bf16[16,64,1024,1]{2,1,0,3:T(8,128)(2,1)S(1)} %bitcast.56, f32[128,16,64]{0,2,1:T(8,128)S(1)} %broadcast_multiply_fusion), kind=kOutput, calls=%fused_computation.5 | convolution fusion | flops 2149515264 | bytes 4980736 | tf_op jit(solution)/shard_map/dot_general | solution.py:26
  42.2 1.0 %fusion.1 = (f32[8]{0:T(128)S(1)}, f32[8192]{0:T(1024)S(1)}, f32[8,8192]{1,0:T(8,128)}) fusion(f32[1,8,64,128]{3,2,1,0:T(8,128)S(1)} %convolution_bitcast_fusion, bf16[8,8192]{1,0:T(8,128)(2,1)S(1)} %copy-done.3), kind=kLoop, calls=%fused_computation.16 | loop fusion | flops 319480 | bytes 688160 | tf_op jit(solution)/shard_map/reduce_sum | solution.py:100
  43.2 1.6 %collective-permute-start.2 = (f32[8192]{0:T(1024)S(1)}, f32[8192]{0:T(1024)S(1)}, u32[]{:S(2)}, u32[]{:S(2)}) collective-permute-start(f32[8192]{0:T(1024)S(1)} %get-tuple-element.4), channel_id=1, source_target_pairs={{0,1},{1,0},{2,3},{3,2},{4,5},{5,4},{6,7},{7,6},{8,9},{9,8},{10,11... | collective-permute-start | bytes 98312 | tf_op jit(solution)/shard_map/ppermute | solution.py:39
  44.8 2.6 %collective-permute-start.1 = (f32[8192]{0:T(1024)S(1)}, f32[8192]{0:T(1024)S(1)}, u32[]{:S(2)}, u32[]{:S(2)}) collective-permute-start(f32[8192]{0:T(1024)S(1)} %get-tuple-element.4), channel_id=1, source_target_pairs={{0,2},{1,3},{2,0},{3,1},{4,6},{5,7},{6,4},{7,5},{8,10},{9,11},{10,... | collective-permute-start | bytes 98312 | tf_op jit(solution)/shard_map/ppermute | solution.py:39
  47.6 1.2 %collective-permute-done.3 = f32[8]{0:T(128)S(1)} collective-permute-done((f32[8]{0:T(128)S(1)}, f32[8]{0:T(128)S(1)}, u32[]{:S(2)}, u32[]{:S(2)}) %collective-permute-start.3) | collective-permute-done | bytes 64 | tf_op jit(solution)/shard_map/ppermute | solution.py:53
  49.3 3.0 %collective-permute-done.4 = f32[8]{0:T(128)S(1)} collective-permute-done((f32[8]{0:T(128)S(1)}, f32[8]{0:T(128)S(1)}, u32[]{:S(2)}, u32[]{:S(2)}) %collective-permute-start.4) | collective-permute-done | bytes 64 | tf_op jit(solution)/shard_map/ppermute | solution.py:53
  52.9 3.0 %collective-permute-done.5 = f32[8]{0:T(128)S(1)} collective-permute-done((f32[8]{0:T(128)S(1)}, f32[8]{0:T(128)S(1)}, u32[]{:S(2)}, u32[]{:S(2)}) %collective-permute-start.5) | collective-permute-done | bytes 64 | tf_op jit(solution)/shard_map/ppermute | solution.py:53
  (50 shorter events, 7.7 us)
Async XLA Ops:
  0.6 18.2 %copy-start = (bf16[128,1024]{1,0:T(8,128)(2,1)S(1)}, bf16[128,1024]{1,0:T(8,128)(2,1)}, u32[]{:S(2)}) copy-start(bf16[128,1024]{1,0:T(8,128)(2,1)} %param.15) | copy-start | bytes 786436
  0.6 10.7 %copy-start.6 = (bf16[128,64]{0,1:T(8,128)(2,1)S(1)}, bf16[128,64]{0,1:T(8,128)(2,1)}, u32[]{:S(2)}) copy-start(bf16[128,64]{0,1:T(8,128)(2,1)} %param.16) | copy-start | bytes 49156
  4.0 9.8 %all-to-all-start = ((s32[8,1,16]{2,1,0:T(1,128)}), s32[8,1,16]{2,1,0:T(1,128)S(1)}, u32[]{:S(2)}, u32[]{:S(2)}) async-start(s32[8,1,16]{2,1,0:T(1,128)} %bitcast.3), calls=%async_computation | async-start | bytes 8192 | tf_op jit(solution)/shard_map/all_to_all | solution.py:78
  15.4 8.0 %all-to-all-start.2 = ((bf16[8,2,512]{2,1,0:T(2,128)(2,1)}), bf16[8,2,512]{2,1,0:T(2,128)(2,1)S(1)}, u32[]{:S(2)}, u32[]{:S(2)}) async-start(bf16[8,2,512]{2,1,0:T(2,128)(2,1)} %reshape.188), calls=%async_computation.2 | async-start | bytes 32768 | tf_op jit(solution)/shard_map/all_to_all | solution.py:85
  18.8 9.0 %copy-start.1 = (bf16[1024,1024]{1,0:T(8,128)(2,1)S(1)}, bf16[1024,1024]{1,0:T(8,128)(2,1)}, u32[]{:S(2)}) copy-start(bf16[1024,1024]{1,0:T(8,128)(2,1)} %param.17) | copy-start | bytes 6291460
  23.5 10.3 %all-to-all-start.1 = ((bf16[8,16,1024]{2,1,0:T(8,128)(2,1)}), bf16[8,16,1024]{2,1,0:T(8,128)(2,1)S(1)}, u32[]{:S(2)}, u32[]{:S(2)}) async-start(bf16[8,16,1024]{2,1,0:T(8,128)(2,1)} %broadcast_select_fusion), calls=%async_computation.1 | async-start | bytes 524288 | tf_op jit(solution)/shard_map/all_to_all | solution.py:84
  27.8 2.5 %copy-start.7 = (s32[128]{0:T(128)S(1)}, s32[128]{0:T(128)}, u32[]{:S(2)}) copy-start(s32[128]{0:T(128)} %param.14) | copy-start | bytes 1540
  34.7 1.7 %copy-start.2 = (bf16[1024,1024]{0,1:T(8,128)(2,1)S(1)}, bf16[1024,1024]{0,1:T(8,128)(2,1)}, u32[]{:S(2)}) copy-start(bf16[1024,1024]{0,1:T(8,128)(2,1)} %copy.58) | copy-start | bytes 6291460
  38.8 2.8 %copy-start.4 = (f32[8192]{0:T(1024)S(1)}, f32[8192]{0:T(1024)}, u32[]{:S(2)}) copy-start(f32[8192]{0:T(1024)} %param.10) | copy-start | bytes 98308
  38.9 2.8 %copy-start.5 = (bf16[128,128]{1,0:T(8,128)(2,1)S(1)}, bf16[128,128]{1,0:T(8,128)(2,1)}, u32[]{:S(2)}) copy-start(bf16[128,128]{1,0:T(8,128)(2,1)} %param.11) | copy-start | bytes 98308
  41.3 0.9 %copy-start.3 = (bf16[8,8192]{1,0:T(8,128)(2,1)S(1)}, bf16[8,8192]{1,0:T(8,128)(2,1)}, u32[]{:S(2)}) copy-start(bf16[8,8192]{1,0:T(8,128)(2,1)} %param.9) | copy-start | bytes 393220
  43.2 13.3 %collective-permute-start.2 = (f32[8192]{0:T(1024)S(1)}, f32[8192]{0:T(1024)S(1)}, u32[]{:S(2)}, u32[]{:S(2)}) collective-permute-start(f32[8192]{0:T(1024)S(1)} %get-tuple-element.4), channel_id=1, source_target_pairs={{0,1},{1,0},{2,3},{3,2},{4,5},{5,4},{6,7},{7,6},{8,9},{9,8},{10,11... | collective-permute-start | bytes 98312 | tf_op jit(solution)/shard_map/ppermute | solution.py:39
  44.8 11.6 %collective-permute-start.1 = (f32[8192]{0:T(1024)S(1)}, f32[8192]{0:T(1024)S(1)}, u32[]{:S(2)}, u32[]{:S(2)}) collective-permute-start(f32[8192]{0:T(1024)S(1)} %get-tuple-element.4), channel_id=1, source_target_pairs={{0,2},{1,3},{2,0},{3,1},{4,6},{5,7},{6,4},{7,5},{8,10},{9,11},{10,... | collective-permute-start | bytes 98312 | tf_op jit(solution)/shard_map/ppermute | solution.py:39
  47.4 9.1 %collective-permute-start = (f32[8192]{0:T(1024)S(1)}, f32[8192]{0:T(1024)S(1)}, u32[]{:S(2)}, u32[]{:S(2)}) collective-permute-start(f32[8192]{0:T(1024)S(1)} %get-tuple-element.4), channel_id=1, source_target_pairs={{0,3},{1,2},{2,1},{3,0},{4,7},{5,6},{6,5},{7,4},{8,11},{9,10},{10,... | collective-permute-start | bytes 98312 | tf_op jit(solution)/shard_map/ppermute | solution.py:39
  47.6 1.2 %collective-permute-start.3 = (f32[8]{0:T(128)S(1)}, f32[8]{0:T(128)S(1)}, u32[]{:S(2)}, u32[]{:S(2)}) collective-permute-start(f32[8]{0:T(128)S(1)} %get-tuple-element.3), channel_id=1, source_target_pairs={{0,4},{4,0},{8,12},{12,8},{16,20},{20,16},{24,28},{28,24},{1,5},{5... | collective-permute-start | bytes 104 | tf_op jit(solution)/shard_map/ppermute | solution.py:53
  48.8 3.6 %collective-permute-start.4 = (f32[8]{0:T(128)S(1)}, f32[8]{0:T(128)S(1)}, u32[]{:S(2)}, u32[]{:S(2)}) collective-permute-start(f32[8]{0:T(128)S(1)} %add.37), channel_id=1, source_target_pairs={{0,8},{4,12},{8,0},{12,4},{16,24},{20,28},{24,16},{28,20},{1,9},{5... | collective-permute-start | bytes 104 | tf_op jit(solution)/shard_map/ppermute | solution.py:53
  52.3 3.6 %collective-permute-start.5 = (f32[8]{0:T(128)S(1)}, f32[8]{0:T(128)S(1)}, u32[]{:S(2)}, u32[]{:S(2)}) collective-permute-start(f32[8]{0:T(128)S(1)} %add.38), channel_id=1, source_target_pairs={{0,16},{4,20},{8,24},{12,28},{16,0},{20,4},{24,8},{28,12},{1,17},{... | collective-permute-start | bytes 104 | tf_op jit(solution)/shard_map/ppermute | solution.py:53
